TPU v7x, 32 devices: a whole 2x2x4 slice. The times are simulated.
32 devices in a mesh: groups: 2 (over y), heads: 4 (over z), batch: 4 (over x, core).
Axes of the slice: x: 2, y: 2, z: 4, core: 2. Of those that a mesh axis runs over, the one named last changes fastest.
Arguments:
- queries: bfloat16 [128, 8192], P(('groups', 'batch'), 'heads'), parts along dimension 0, may hold values from -110 to 110
- new_kv: bfloat16 [16, 64, 256], P(('groups', 'heads'), 'batch'), parts along dimension 0, may hold values from -15 to 15
- kv_pool: bfloat16 [16, 192, 128, 256], P(('groups', 'heads'), 'batch'), parts along dimension 0, may hold values from -6 to 6
- page_counts: int32 [8, 16], P(('groups', 'batch')), parts along dimension 0, may hold values from 1 to 6, 48 in all within a row
- last_fill: int32 [8, 16], P(('groups', 'batch')), parts along dimension 0, may hold values from 1 to 128
- page_order: int32 [8, 48], P(('groups', 'batch')), parts along dimension 0, may hold values from 0 to 47, each once within a row
- hidden: bfloat16 [128, 8192], P(('groups', 'batch')), parts along dimension 0, may hold values from -0.59765625 to 0.59765625
- out_weight: bfloat16 [8192, 8192], P('heads'), may hold values from -0.5 to 0.5
- norm_gain: bfloat16 [8192], replicated, may hold values from 0.099609375 to 1.8984375
- sectioned: bfloat16 [8, 4, 8, 128, 256], P(('groups', 'heads'), 'batch'), parts along dimension 0, may hold values from -6 to 6
- routes: int32 [8, 4, 8, 1], P(('groups', 'heads'), 'batch'), parts along dimension 0, may hold values from 0 to 7; in each aligned block of 8 rows (0 to 7, 8 to 15, ..., all dimensions but the last counted through in order) at most 2 rows name the same one
Outputs:
- residual_out: bfloat16 [128, 8192], P(('groups', 'batch')), parts along dimension 0
- normed: bfloat16 [128, 8192], P(('groups', 'batch')), parts along dimension 0
- arrival: bfloat16 [16, 4, 4, 2, 128, 256], P(('groups', 'heads'), 'batch'), parts along dimension 0
There are 2 independent parts, one for each index of `groups`. A program takes and returns all parts, laid end to end along the dimension named above; an argument that names none is the same for every part. Nothing has to cross between parts.
Inputs may be any that keep to these rules, and one draw needn't show every extreme that they name: `routes`: every key-value head is named by at most 2 sectioned pages of one device. `page_counts`: the page counts of one batch owner sum to 48.
All inputs are finite; a program needn't handle non-finite values.
Results may differ from a plain program's by a relative error of at most 0.0066.
Values may be sent and summed in bfloat16 or wider, within the bound.
A program may use at most 128 MiB of HBM per device.

v0:
```python
import jax
import jax.numpy as jnp
from jax import lax
from jax.sharding import PartitionSpec as P

KV_HEADS = 8
PER_HEAD_CAP = 2


norm_epsilon = 1e-06


def attend(queries, new_kv, kv_pool, counts, fill, order):
    slot_count, pool_pages, page_size, lane_width = kv_pool.shape
    head_dim = lane_width // 2
    requests = queries.shape[0]
    score_scale = 1.0 / head_dim**0.5
    position = jnp.arange(pool_pages, dtype=jnp.int32)
    position_in_order = jnp.sum(
        jnp.where(order[None, :] == position[:, None], position[None, :], 0), axis=1
    )
    count_ends = jnp.cumsum(counts)
    starts = count_ends - counts
    owner_index = jnp.sum(
        (count_ends[None, :] <= position_in_order[:, None]).astype(jnp.int32), axis=1
    )
    member = owner_index[:, None] == jnp.arange(requests, dtype=jnp.int32)[None, :]
    member_float = member.astype(jnp.float32)
    within = position_in_order - jnp.sum(jnp.where(member, starts[None, :], 0), axis=1)
    context = (counts - 1) * page_size + fill
    context_limit = jnp.sum(jnp.where(member, context[None, :], 0), axis=1)
    live_tokens = (
        within[:, None] * page_size + jnp.arange(page_size, dtype=jnp.int32)[None, :]
        < context_limit[:, None]
    )
    page_queries = jnp.einsum(
        "pr,rlgd->lpgd", member.astype(jnp.bfloat16), queries, preferred_element_type=jnp.float32
    ).astype(jnp.bfloat16)
    scores = (
        jnp.einsum(
            "lpgd,lptd->lpgt",
            page_queries,
            kv_pool[..., :head_dim],
            preferred_element_type=jnp.float32,
        )
        * score_scale
    )
    scores = jnp.where(live_tokens[None, :, None, :], scores, -1e30)
    page_top = jnp.max(scores, axis=3)
    fresh_score = (
        jnp.einsum(
            "rlgd,lrd->lrg", queries, new_kv[..., :head_dim], preferred_element_type=jnp.float32
        )
        * score_scale
    )
    masked_top = jnp.where(member.T[None, :, :, None], page_top[:, None, :, :], -1e30)
    request_top = jnp.maximum(fresh_score, jnp.max(masked_top, axis=2))
    page_ref = jnp.einsum("pr,lrg->lpg", member_float, request_top, precision=lax.Precision.HIGHEST)
    weight = jnp.where(live_tokens[None, :, None, :], jnp.exp(scores - page_ref[..., None]), 0.0)
    page_den = jnp.sum(weight, axis=3)
    page_num = jnp.einsum(
        "lpgt,lptd->lpgd",
        weight.astype(jnp.bfloat16),
        kv_pool[..., head_dim:],
        preferred_element_type=jnp.float32,
    )
    fresh_weight = jnp.exp(fresh_score - request_top)
    fresh_rounded = lax.optimization_barrier(fresh_weight.astype(jnp.bfloat16)).astype(jnp.float32)
    denominator = (
        jnp.einsum("pr,lpg->lrg", member_float, page_den, precision=lax.Precision.HIGHEST)
        + fresh_weight
    )
    numerator = jnp.einsum("pr,lpgd->lrgd", member_float, page_num, precision=lax.Precision.HIGHEST)
    numerator = numerator + fresh_rounded[..., None] * new_kv[:, :, None, head_dim:].astype(
        jnp.float32
    )
    attended = numerator / denominator[..., None]
    attended = jnp.transpose(attended, (1, 0, 2, 3)).astype(jnp.bfloat16)
    return attended.reshape(requests, -1)


def landing_table(destination, head_total, most_pages):
    sectioned_count = destination.shape[0]
    order_ids = jnp.arange(sectioned_count, dtype=jnp.int32)
    same_head = destination[:, None] == destination[None, :]
    earlier = order_ids[:, None] > order_ids[None, :]
    page_rank = jnp.sum((same_head & earlier).astype(jnp.int32), axis=1)
    matches = (
        destination[None, None, :] == jnp.arange(head_total, dtype=jnp.int32)[:, None, None]
    ) & (page_rank[None, None, :] == jnp.arange(most_pages, dtype=jnp.int32)[None, :, None])
    source_index = jnp.sum(jnp.where(matches, order_ids[None, None, :], 0), axis=2)
    source_valid = jnp.any(matches, axis=2)
    return (source_index, source_valid)


def per_device(
    queries,
    new_kv,
    kv_pool,
    page_counts,
    last_fill,
    page_order,
    hidden,
    out_weight,
    norm_gain,
    sectioned,
    routes,
):
    head_count = lax.axis_size("heads")
    slots_dev = new_kv.shape[0]
    head_dim = kv_pool.shape[3] // 2
    requests = hidden.shape[0]
    group_size = queries.shape[1] // (slots_dev * head_dim)
    page_data = sectioned[0, 0]
    source_index, source_valid = landing_table(routes[0, 0, :, 0], KV_HEADS, PER_HEAD_CAP)
    cache_total = head_count * slots_dev
    target = (
        (
            jnp.arange(head_count, dtype=jnp.int32)[None, :] * slots_dev
            + jnp.arange(slots_dev, dtype=jnp.int32)[:, None]
        )
        * KV_HEADS
        // cache_total
    )
    picked = source_index[target]
    present = source_valid[target]
    outgoing = page_data[picked]
    outgoing = jnp.where(present[..., None, None], outgoing, jnp.zeros_like(outgoing))
    landed = lax.all_to_all(outgoing, "heads", split_axis=1, concat_axis=1, tiled=True)
    arrival = landed[:, None]
    query_block = queries.reshape(requests, slots_dev, group_size, head_dim)
    attn = attend(query_block, new_kv, kv_pool, page_counts[0], last_fill[0], page_order[0])
    partial_terms = jnp.dot(attn, out_weight, preferred_element_type=jnp.float32)
    summed = lax.psum(partial_terms, "heads")
    mixed = hidden.astype(jnp.float32) + summed
    mean_square = jnp.mean(mixed * mixed, axis=1, keepdims=True)
    normed = (mixed * lax.rsqrt(mean_square + norm_epsilon) * norm_gain.astype(jnp.float32)).astype(
        jnp.bfloat16
    )
    residual_out = mixed.astype(jnp.bfloat16)
    return (residual_out, normed, arrival)


def solution(mesh):
    return jax.shard_map(
        per_device,
        mesh=mesh,
        in_specs=(
            P(("groups", "batch"), "heads"),
            P(("groups", "heads"), "batch", None),
            P(("groups", "heads"), "batch", None, None),
            P(("groups", "batch"), None),
            P(("groups", "batch"), None),
            P(("groups", "batch"), None),
            P(("groups", "batch"), None),
            P("heads", None),
            P(),
            P(("groups", "heads"), "batch", None, None, None),
            P(("groups", "heads"), "batch", None, None),
        ),
        out_specs=(
            P(("groups", "batch"), None),
            P(("groups", "batch"), None),
            P(("groups", "heads"), "batch", None, None, None, None),
        ),
        check_vma=False,
    )
```

profile of v0, /device:TPU:0, one launch (start us, length us, event | category | flops | bytes accessed | tf_op | source)
XLA Modules:
  0.0 96.6 jit_solution(1213633889777169506)
XLA Ops:
  7.2 0.0 copy-start
  7.2 0.0 all-reduce.2.cloned.1.call-start
  7.2 0.8 select_reduce_fusion.1
  8.0 0.7 copy.69
  8.8 0.1 reduce
  8.9 0.1 convert_reduce_fusion
  9.0 0.7 add_bitcast_fusion
  9.7 0.1 select_reduce_fusion.3
  9.8 0.7 convert_bitcast_fusion
  10.5 0.8 copy.93
  11.4 0.3 fusion.10
  11.6 0.1 fusion.27
  11.8 0.1 copy.90
  11.9 0.1 add_compare_fusion
  12.0 3.7 %fusion.48 = (f32[2,48,8]{2,1,0:T(8,128)S(1)}, f32[2,48,8,128]{3,2,1,0:T(8,128)S(1)}) fusion(bf16[2,48,128,256]{3,2,1,0:T(8,128)(2,1)} %param.13, bf16[2,48,8,128]{3,1,2,0:T(8,128)(2,1)S(1)} %fusion.10, pred[48,128]{1,0:T(8,128)(4,1)S(1)} %add_compare_fusion), kind=kOutput, calls=%fused_computation.86 | convolution fusion | flops 25459968 | bytes 3744768 | tf_op jit(solution)/shard_map/lpgd,lptd->lpgt/dot_general | solution.py:40
  15.7 0.1 copy.72
  15.7 0.1 select_reduce_fusion
  15.9 0.1 copy.73
  15.9 0.1 convolution_bitcast_fusion.1
  16.1 0.1 copy.74
  16.2 0.3 fusion.15
  16.5 2.9 %fusion = f32[2,48,8,128]{3,2,1,0:T(8,128)S(1)} fusion(bf16[2,48,128,256]{3,2,1,0:T(8,128)(2,1)} %param.13, f32[2,48,8,128]{3,2,1,0:T(8,128)S(1)} %get-tuple-element.24, f32[2,48,8]{2,1,0:T(8,128)S(1)} %copy.74, pred[48,128]{1,0:T(8,128)(4,1)S(1)} %add_compare_fusion), kind=kOutput, calls=%fused_computation.3 | convolution fusion | flops 25460736 | bytes 3941376 | tf_op jit(solution)/shard_map/lpgt,lptd->lpgd/dot_general | solution.py:61
  19.3 0.1 copy.76
  19.4 0.1 fusion.13
  19.6 0.3 fusion.12
  19.9 0.0 copy-start.3
  19.9 13.7 %fusion.23 = f32[16,8192]{1,0:T(8,128)} fusion(bf16[2048,8192]{1,0:T(8,128)(2,1)} %param.18, bf16[2,8,16,128]{3,2,1,0:T(8,128)(2,1)S(1)} %bitcast.73), kind=kOutput, calls=%fused_computation.31 | convolution fusion | flops 536870912 | bytes 34144256 | tf_op jit(solution)/shard_map/dot_general | solution.py:133
  33.6 0.0 copy-start.2
  33.6 0.0 copy-start.1
  33.6 0.0 all-reduce.2.cloned.1.call-update
  33.6 0.0 copy-done.3
  33.6 0.2 convert_reduce_fusion.1
  33.8 0.1 and_reduce_fusion
  34.0 0.2 fusion.30
  34.2 0.1 reshape.257
  34.2 0.1 copy.79
  34.3 0.1 copy.82
  34.4 0.6 gather_fusion.1
  35.0 0.6 gather_fusion
  35.6 0.1 copy.92
  35.7 0.1 copy.84
  35.8 0.1 reshape.273
  35.9 0.0 copy-done
  35.9 0.6 gather_fusion.2
  36.5 0.1 broadcast_select_fusion
  36.6 1.1 %copy.85 = bf16[2,4,2,128,256]{4,3,2,0,1:T(8,128)(2,1)} copy(bf16[2,4,2,128,256]{4,3,2,1,0:T(8,128)(2,1)S(1)} %broadcast_select_fusion) | data formatting | bytes 2097152 | tf_op jit(solution)/shard_map/jit(_where)/select_n | solution.py:128
  37.7 6.3 %all-to-all-start = ((bf16[2,4,2,128,256]{4,3,2,0,1:T(8,128)(2,1)}), bf16[2,4,2,128,256]{4,3,2,0,1:T(8,128)(2,1)S(1)}, u32[]{:S(2)}, u32[]{:S(2)}) async-start(bf16[2,4,2,128,256]{4,3,2,0,1:T(8,128)(2,1)} %copy.85), calls=%async_computation | async-start | bytes 2097152 | tf_op jit(solution)/shard_map/all_to_all | solution.py:129
  44.0 0.0 copy-done.2
  44.1 41.5 %all-reduce.2.cloned.1.call-done = f32[16,8192]{1,0:T(8,128)} async-done(((f32[16,8192]{1,0:T(8,128)}), f32[16,8192]{1,0:T(8,128)}) %all-reduce.2.cloned.1.call-update) | async-done | bytes 524304 | tf_op jit(solution)/shard_map/psum | solution.py:134
  85.6 0.0 copy-done.1
  85.6 1.2 %multiply_reduce_fusion = f32[16]{0:T(128)S(1)} fusion(f32[16,8192]{1,0:T(8,128)} %all-reduce.2.cloned.1.call-done, bf16[16,8192]{1,0:T(8,128)(2,1)S(1)} %copy-done.1), kind=kLoop, calls=%fused_computation.19 | loop fusion | flops 524272 | bytes 786496 | tf_op jit(solution)/shard_map/reduce_sum | solution.py:136
  86.8 1.9 %multiply_convert_fusion = (bf16[16,8192]{1,0:T(8,128)(2,1)}, bf16[16,8192]{1,0:T(8,128)(2,1)}) fusion(f32[8192]{0:T(1024)S(1)} %convert_element_type.46, f32[16]{0:T(128)S(1)} %add_rsqrt_fusion, f32[16,8192]{1,0:T(8,128)} %all-reduce.2.cloned.1.call-done, bf16[16,8192]{1,0:T(8,128)(2,1)S(1)} %copy-done.1), kind=kLoop, calls=%fused_computation.18 | loop fusion | flops 786432 | bytes 1343552 | tf_op jit(solution)/shard_map/convert_element_type | solution.py:137
  88.7 0.0 all-to-all-done
  88.7 1.0 %copy.86 = bf16[2,1,4,2,128,256]{5,4,3,2,1,0:T(8,128)(2,1)} copy(bf16[2,1,4,2,128,256]{5,4,3,0,2,1:T(8,128)(2,1)S(1)} %bitcast.71) | data formatting | bytes 2097152
  (15 shorter events, 0.1 us)
Async XLA Ops:
  7.2 28.7 %copy-start = (bf16[1,1,8,128,256]{4,3,2,1,0:T(8,128)(2,1)S(1)}, bf16[1,1,8,128,256]{4,3,2,1,0:T(8,128)(2,1)}, u32[]{:S(2)}) copy-start(bf16[1,1,8,128,256]{4,3,2,1,0:T(8,128)(2,1)} %param.20) | copy-start | bytes 1572868
  7.2 78.4 %all-reduce.2.cloned.1.call-start = ((), (), s32[]{:S(2)}) async-start(), calls=%async_computation.1 | async-start | bytes 1048576 | tf_op jit(solution)/shard_map/psum | solution.py:134
  19.9 13.7 %copy-start.3 = (s32[1,1,8,1]{2,3,1,0:T(1,128)S(1)}, s32[1,1,8,1]{2,3,1,0:T(1,128)}, u32[]{:S(2)}) copy-start(s32[1,1,8,1]{2,3,1,0:T(1,128)} %param.21) | copy-start | bytes 100
  33.6 10.5 %copy-start.2 = (bf16[8192]{0:T(1024)(128)(2,1)S(1)}, bf16[8192]{0:T(1024)(128)(2,1)}, u32[]{:S(2)}) copy-start(bf16[8192]{0:T(1024)(128)(2,1)} %param.19) | copy-start | bytes 49156
  33.6 52.0 %copy-start.1 = (bf16[16,8192]{1,0:T(8,128)(2,1)S(1)}, bf16[16,8192]{1,0:T(8,128)(2,1)}, u32[]{:S(2)}) copy-start(bf16[16,8192]{1,0:T(8,128)(2,1)} %param.17) | copy-start | bytes 786436
  37.7 51.0 %all-to-all-start = ((bf16[2,4,2,128,256]{4,3,2,0,1:T(8,128)(2,1)}), bf16[2,4,2,128,256]{4,3,2,0,1:T(8,128)(2,1)S(1)}, u32[]{:S(2)}, u32[]{:S(2)}) async-start(bf16[2,4,2,128,256]{4,3,2,0,1:T(8,128)(2,1)} %copy.85), calls=%async_computation | async-start | bytes 2097152 | tf_op jit(solution)/shard_map/all_to_all | solution.py:129
Sparse Core Ops, SparseCore 0:
  33.7 51.7 all-reduce.1
where the time goes:
time: 97.1 us; the launch traced here: 96.6 us
  waiting for transfers between devices  41.5 us (43%)
  matrix products  21.2 us (22%)
  between operations  14.2 us (15%)
  other arithmetic  6.9 us (7%)
  local copies, waits for them, and re-layouts  6.39 us (7%)
  starting transfers between devices  6.38 us (7%)
    psum x1, waiting for transfers between devices, per_device(): summed = lax.psum(partial_terms, 'heads')  41.5 us
    dot_general x1, matrix products, per_device(): jnp.dot(attn, out_weight, preferred_element_type=jnp.float32)  13.7 us
    all_to_all x1, starting transfers between devices, per_device(): lax.all_to_all(outgoing, 'heads', split_axis=1, concat_axis=1, tiled=True)  6.35 us
    dot_general x1, matrix products, attend(): jnp.einsum('lpgd,lptd->lpgt', page_queries, kv_pool[..., :head_dim], pref...  3.69 us
    dot_general x1, matrix products, attend(): jnp.einsum('lpgt,lptd->lpgd', weight.astype(jnp.bfloat16), kv_pool[..., h...  2.86 us
  transfers between devices with their start and end apart: 2, of which 1 were waited for; matrix products, arithmetic and copies ran while one was open for 7% of the time, Pallas kernels for 0%

commit v1 on v0

v1 whole, which is shorter than its diff:
```python
import functools

import jax
import jax.numpy as jnp
from jax import lax
from jax.experimental import pallas as pl
from jax.experimental.pallas import tpu as pltpu
from jax.sharding import PartitionSpec as P

KV_HEADS = 8
MAX_PAGES = 6

norm_epsilon = 1e-06
MESH = pl.DeviceIdType.MESH
CHUNK = 1024
UNROLL = 2


def step_kernel(
    n,
    counts,
    fill,
    order,
    routes,
    queries,
    new_kv,
    kv_pool,
    hidden,
    weight,
    gain,
    sectioned,
    residual_out,
    normed_out,
    arrival,
    sect_v,
    outgoing,
    q_raw,
    q_rows,
    new_raw,
    new_rows,
    kv_v,
    hidden_v,
    gain_v,
    weight_v,
    attn_rows,
    attn_v,
    own_sum,
    terms,
    landed,
    gathered,
    load_sems,
    kv_sems,
    weight_sems,
    own_sems,
    page_send,
    page_recv,
    term_send,
    term_recv,
    block_send,
    block_recv,
):
    me = lax.axis_index("heads")
    slots, pool_pages, page_size, width = kv_v.shape
    head_dim = width // 2
    requests = q_raw.shape[0]
    group = q_rows.shape[2]
    pages = sect_v.shape[0] - 1
    cap = outgoing.shape[2]
    block = terms.shape[2]
    chunk_total, _, chunk = weight_v.shape
    chunks = block // chunk

    def peer(step):
        return lax.rem(me + 1 + step, n)

    def source(step):
        return lax.rem(me + n - 1 - step, n)

    loads = [
        pltpu.make_async_copy(src, dst, load_sems.at[i])
        for i, (src, dst) in enumerate(
            (
                (sectioned.at[0, 0], sect_v.at[pl.ds(0, pages)]),
                (queries, q_raw),
                (new_kv, new_raw),
                (hidden, hidden_v),
                (gain, gain_v),
            )
        )
    ]
    for load in loads[:3]:
        load.start()
    kv_loads = [
        pltpu.make_async_copy(kv_pool.at[l], kv_v.at[l], kv_sems.at[l]) for l in range(slots)
    ]
    for load in kv_loads:
        load.start()

    def weight_load(i):
        column = peer(i // chunks) * block + (i % chunks) * chunk
        return pltpu.make_async_copy(
            weight.at[:, pl.ds(pl.multiple_of(column, chunk), chunk)],
            weight_v.at[i],
            weight_sems.at[i],
        )

    for load in loads[3:]:
        load.start()
    for i in range(chunk_total):
        weight_load(i).start()

    barrier = pltpu.get_barrier_semaphore()
    for step in range(n - 1):
        pl.semaphore_signal(
            barrier, inc=1, device_id={"heads": peer(step)}, device_id_type=MESH
        )

    sect_v[pages] = jnp.zeros(sect_v.shape[1:], sect_v.dtype)
    loads[0].wait()
    page_heads = [routes[0, j] for j in range(pages)]

    def fill_outgoing(step):
        target = peer(step)
        for l in range(slots):
            head = (target * slots + l) * KV_HEADS // (n * slots)
            found = jnp.int32(0)
            picks = [jnp.int32(pages)] * cap
            for j in range(pages):
                hit = page_heads[j] == head
                for k in range(cap):
                    picks[k] = jnp.where(hit & (found == k), j, picks[k])
                found = found + jnp.where(hit, 1, 0)
            for k in range(cap):
                outgoing[step, l, k] = sect_v[picks[k]]

    def page_copy(step, l, place):
        return pltpu.make_async_remote_copy(
            src_ref=outgoing.at[step, l],
            dst_ref=arrival.at[l, 0, place],
            send_sem=page_send.at[step, l],
            recv_sem=page_recv.at[step, l],
            device_id={"heads": peer(step)},
            device_id_type=MESH,
        )

    for step in range(n - 1):
        fill_outgoing(step)
        if step == 0:
            pl.semaphore_wait(barrier, n - 1)
        for l in range(slots):
            page_copy(step, l, me).start()
    fill_outgoing(n - 1)
    own_copies = [
        pltpu.make_async_copy(outgoing.at[n - 1, l], arrival.at[l, 0, me], own_sems.at[l])
        for l in range(slots)
    ]
    for copy in own_copies:
        copy.start()

    loads[1].wait()
    loads[2].wait()
    new_rows[...] = new_raw[...].astype(jnp.float32)
    for l in range(slots):
        for g in range(group):
            first = (l * group + g) * head_dim
            q_rows[l, :, g, :] = q_raw[:, first : first + head_dim].astype(jnp.float32)
    for load in kv_loads:
        load.wait()

    score_scale = 1.0 / head_dim**0.5

    def attend(i, start):
        for sub in range(UNROLL):
            r = i * UNROLL + sub
            count = counts[0, r]
            context = (count - 1) * page_size + fill[0, r]
            picked = [
                order[0, jnp.minimum(start + j, pool_pages - 1)] for j in range(MAX_PAGES)
            ]
            live = (
                lax.broadcasted_iota(jnp.int32, (group, MAX_PAGES * page_size), 1) < context
            )
            for l in range(slots):
                query = q_rows[l, r]
                fresh = new_rows[l, pl.ds(r, 1), :]
                keys = jnp.concatenate([kv_v[l, p, :, :head_dim] for p in picked], axis=0)
                scores = (
                    lax.dot_general(
                        query.astype(jnp.bfloat16),
                        keys,
                        (((1,), (1,)), ((), ())),
                        preferred_element_type=jnp.float32,
                    )
                    * score_scale
                )
                scores = jnp.where(live, scores, -1e30)
                fresh_score = (
                    jnp.sum(query * fresh[:, :head_dim], axis=1, keepdims=True) * score_scale
                )
                top = jnp.maximum(jnp.max(scores, axis=1, keepdims=True), fresh_score)
                w = jnp.where(live, jnp.exp(scores - top), 0.0)
                fresh_w = jnp.exp(fresh_score - top)
                den = jnp.sum(w, axis=1, keepdims=True) + fresh_w
                values = jnp.concatenate([kv_v[l, p, :, head_dim:] for p in picked], axis=0)
                num = jnp.dot(w.astype(jnp.bfloat16), values, preferred_element_type=jnp.float32)
                num = num + fresh_w.astype(jnp.bfloat16).astype(jnp.float32) * fresh[:, head_dim:]
                attn_rows[l, r] = num / den
            start = start + count
        return start

    lax.fori_loop(0, requests // UNROLL, attend, jnp.int32(0))
    for l in range(slots):
        for g in range(group):
            first = (l * group + g) * head_dim
            attn_v[:, first : first + head_dim] = attn_rows[l, :, g, :].astype(jnp.bfloat16)

    def term_copy(step):
        return pltpu.make_async_remote_copy(
            src_ref=terms.at[step],
            dst_ref=landed.at[step],
            send_sem=term_send.at[step],
            recv_sem=term_recv.at[step],
            device_id={"heads": peer(step)},
            device_id_type=MESH,
        )

    def project(step, carry):
        for part in range(chunks):
            i = step * chunks + part
            weight_load(i).wait()
            term = jnp.dot(attn_v[...], weight_v[i], preferred_element_type=jnp.float32)
            own_sum[:, part * chunk : (part + 1) * chunk] = term
            terms[step, :, part * chunk : (part + 1) * chunk] = term.astype(jnp.bfloat16)

        @pl.when(step < n - 1)
        def _():
            term_copy(step).start()

        return carry

    lax.fori_loop(0, n, project, 0)
    loads[3].wait()
    loads[4].wait()

    column = pl.multiple_of(me * block, block)
    total = own_sum[...] + hidden_v[:, pl.ds(column, block)].astype(jnp.float32)
    for step in range(n - 1):
        term_copy(step).wait_recv()
        total = total + landed[step].astype(jnp.float32)
    gathered[me] = total.astype(jnp.bfloat16)

    def block_copy(step, place):
        return pltpu.make_async_remote_copy(
            src_ref=gathered.at[place],
            dst_ref=gathered.at[place],
            send_sem=block_send.at[step],
            recv_sem=block_recv.at[step],
            device_id={"heads": peer(step)},
            device_id_type=MESH,
        )

    for step in range(n - 1):
        block_copy(step, me).start()
    for step in range(n - 1):
        term_copy(step).wait_send()
    for step in range(n - 1):
        block_copy(step, source(step)).wait_recv()
    square = jnp.zeros((requests, 1), jnp.float32)
    for c in range(n):
        mixed = gathered[c].astype(jnp.float32)
        square = square + jnp.sum(mixed * mixed, axis=1, keepdims=True)
    factor = lax.rsqrt(square / (n * block) + norm_epsilon)
    for c in range(n):
        piece = gathered[c]
        here = slice(c * block, (c + 1) * block)
        residual_out[:, here] = piece
        normed_out[:, here] = (
            piece.astype(jnp.float32) * factor * gain_v[:, here].astype(jnp.float32)
        ).astype(jnp.bfloat16)

    for step in range(n - 1):
        block_copy(step, me).wait_send()
        for l in range(slots):
            page_copy(step, l, me).wait_send()
            page_copy(step, l, source(step)).wait_recv()
    for copy in own_copies:
        copy.wait()


def per_device(
    queries,
    new_kv,
    kv_pool,
    page_counts,
    last_fill,
    page_order,
    hidden,
    out_weight,
    norm_gain,
    sectioned,
    routes,
    *,
    cap,
):
    n = lax.axis_size("heads")
    slots, pool_pages, page_size, width = kv_pool.shape
    head_dim = width // 2
    requests, model = hidden.shape
    rows = out_weight.shape[0]
    group = rows // (slots * head_dim)
    pages = sectioned.shape[2]
    block = model // n
    chunk = min(CHUNK, block)
    bf16, f32 = jnp.bfloat16, jnp.float32
    dma = pltpu.SemaphoreType.DMA
    smem = pl.BlockSpec(memory_space=pltpu.SMEM)
    hbm = pl.BlockSpec(memory_space=pl.ANY)
    vmem = pl.BlockSpec(memory_space=pltpu.VMEM)
    return pl.pallas_call(
        functools.partial(step_kernel, n),
        out_shape=(
            jax.ShapeDtypeStruct((requests, model), bf16),
            jax.ShapeDtypeStruct((requests, model), bf16),
            jax.ShapeDtypeStruct((slots, 1, n, cap, page_size, width), bf16),
        ),
        in_specs=[smem] * 4 + [hbm] * 7,
        out_specs=(vmem, vmem, hbm),
        scratch_shapes=[
            pltpu.VMEM((pages + 1, page_size, width), bf16),
            pltpu.VMEM((n, slots, cap, page_size, width), bf16),
            pltpu.VMEM((requests, rows), bf16),
            pltpu.VMEM((slots, requests, group, head_dim), f32),
            pltpu.VMEM((slots, requests, width), bf16),
            pltpu.VMEM((slots, requests, width), f32),
            pltpu.VMEM((slots, pool_pages, page_size, width), bf16),
            pltpu.VMEM((requests, model), bf16),
            pltpu.VMEM((1, model), bf16),
            pltpu.VMEM((model // chunk, rows, chunk), bf16),
            pltpu.VMEM((slots, requests, group, head_dim), f32),
            pltpu.VMEM((requests, rows), bf16),
            pltpu.VMEM((requests, block), f32),
            pltpu.VMEM((n, requests, block), bf16),
            pltpu.VMEM((n - 1, requests, block), bf16),
            pltpu.VMEM((n, requests, block), bf16),
            dma((5,)),
            dma((slots,)),
            dma((model // chunk,)),
            dma((slots,)),
            dma((n - 1, slots)),
            dma((n - 1, slots)),
            dma((n - 1,)),
            dma((n - 1,)),
            dma((n - 1,)),
            dma((n - 1,)),
        ],
        compiler_params=pltpu.CompilerParams(
            collective_id=0, has_side_effects=True, vmem_limit_bytes=60 * 1024 * 1024
        ),
        name="decode_step",
    )(
        page_counts,
        last_fill,
        page_order,
        routes.reshape(1, pages),
        queries,
        new_kv,
        kv_pool,
        hidden,
        out_weight,
        norm_gain.reshape(1, model),
        sectioned,
    )


PER_HEAD_CAP = 2


def solution(mesh):
    return jax.shard_map(
        functools.partial(per_device, cap=PER_HEAD_CAP),
        mesh=mesh,
        in_specs=(
            P(("groups", "batch"), "heads"),
            P(("groups", "heads"), "batch", None),
            P(("groups", "heads"), "batch", None, None),
            P(("groups", "batch"), None),
            P(("groups", "batch"), None),
            P(("groups", "batch"), None),
            P(("groups", "batch"), None),
            P("heads", None),
            P(),
            P(("groups", "heads"), "batch", None, None, None),
            P(("groups", "heads"), "batch", None, None),
        ),
        out_specs=(
            P(("groups", "batch"), None),
            P(("groups", "batch"), None),
            P(("groups", "heads"), "batch", None, None, None, None),
        ),
        check_vma=False,
    )
```

time: 97.1 us -> 52.6 us (0.54)
  Pallas kernels: 0 us -> 44.7 us
  waiting for transfers between devices: 41.5 us -> 0 us
  matrix products: 21.2 us -> 0 us
  between operations: 14.2 us -> 0.64 us
  other arithmetic: 6.9 us -> 0 us
  starting transfers between devices: 6.38 us -> 0 us
    pallas_call x0 -> x1, Pallas kernels: none -> 44.7 us  [per_device(): pl.pallas_call(functools.partial(step_kernel, n), out_shape=(jax.ShapeDty...]
    psum x1 -> x0, waiting for transfers between devices: 41.5 us -> none  [per_device(): summed = lax.psum(partial_terms, 'heads')]
    dot_general x7 -> x0, matrix products: 21.1 us -> none  [the longest x1 13.7 us: per_device(): jnp.dot(attn, out_weight, preferred_element_type=jnp.float32)]
    all_to_all x1 -> x0, starting transfers between devices: 6.35 us -> none  [per_device(): lax.all_to_all(outgoing, 'heads', split_axis=1, concat_axis=1, tiled=True)]
    unnamed x10 -> x3, local copies, waits for them, and re-layouts: 1.92 us -> 5.62 us
    reduce_sum x7 -> x0, other arithmetic: 2.85 us -> none  [the longest x1 1.22 us: per_device(): mean_square = jnp.mean(mixed * mixed, axis=1, keepdims=True)]
    convert_element_type x3 -> x0, other arithmetic: 1.91 us -> none  [the longest x1 1.89 us: per_device(): (mixed * lax.rsqrt(mean_square + norm_epsilon) * norm_gain.astype(jnp.flo...]
    gather x4 -> x0, local copies, waits for them, and re-layouts: 1.84 us -> none  [the longest x2 0.66 us: per_device(): picked = source_index[target]]
  transfers between devices with their start and end apart: 2 -> 0, of which waited for: 1 -> 0; matrix products, arithmetic and copies ran while one was open for 7% -> 0% of each run, Pallas kernels for 0% -> 0%
where the time goes in v1:
time: 52.6 us; the launch traced here: 52.4 us
  Pallas kernels  44.7 us (85%)
  local copies, waits for them, and re-layouts  6.98 us (13%)
  between operations  0.64 us (1%)
    pallas_call x1, Pallas kernels, per_device(): pl.pallas_call(functools.partial(step_kernel, n), out_shape=(jax.ShapeDty...  44.7 us
    unnamed x3, local copies, waits for them, and re-layouts  5.62 us
    reshape x1, local copies, waits for them, and re-layouts, per_device(): norm_gain.reshape(1, model)  1.35 us

profile of v1, /device:TPU:0, one launch (start us, length us, event | category | flops | bytes accessed | tf_op | source)
XLA Modules:
  0.0 52.4 jit_solution(16921473402854806148)
XLA Ops:
  0.6 1.4 %reshape.13.gain = bf16[1,8192]{1,0:T(2,128)(2,1)} reshape(bf16[8192]{0:T(1024)(128)(2,1)} %param.19) | data formatting | bytes 32768 | tf_op jit(solution)/shard_map/reshape | solution.py:370
  2.0 44.7 %decode_step.1 = (bf16[16,8192]{1,0:T(8,128)(2,1)}, bf16[16,8192]{1,0:T(8,128)(2,1)}, bf16[2,1,4,2,128,256]{5,4,3,2,1,0:T(8,128)(2,1)}) custom-call(s32[1,16]{1,0:T(1,128)} %counts.1, s32[1,16]{1,0:T(1,128)} %fill.1, s32[1,48]{1,0:T(1,128)} %order.1, s32[1,8]{1,0:T(1,128)} %bitcast.1, bf16[16,2048]{1,0:T(8,128)(2,1)} %queries.1, bf16[2,16,256]{2,1,0:T(8,128)(2,1)} %new_kv.1, ...), custom_call_target="tpu_custom_call" | custom-call | tf_op jit(solution)/shard_map/decode_step/pallas_call | solution.py:319
  46.7 1.7 %copy.17 = bf16[16,8192]{1,0:T(8,128)(2,1)} copy(bf16[16,8192]{1,0:T(8,128)(2,1)} %get-tuple-element.6) | data formatting | bytes 524288
  48.4 1.7 %copy.18 = bf16[16,8192]{1,0:T(8,128)(2,1)} copy(bf16[16,8192]{1,0:T(8,128)(2,1)} %get-tuple-element.7) | data formatting | bytes 524288
  50.1 2.3 %copy.19 = bf16[2,1,4,2,128,256]{5,4,3,2,1,0:T(8,128)(2,1)} copy(bf16[2,1,4,2,128,256]{5,4,3,2,1,0:T(8,128)(2,1)} %get-tuple-element.8) | data formatting | bytes 2097152

commit v2 on v1

v2 whole, which is shorter than its diff:
```python
import functools

import jax
import jax.numpy as jnp
from jax import lax
from jax.experimental import pallas as pl
from jax.experimental.pallas import tpu as pltpu
from jax.sharding import PartitionSpec as P

KV_HEADS = 8
MAX_PAGES = 6

norm_epsilon = 1e-06
MESH = pl.DeviceIdType.MESH
CHUNK = 1024
UNROLL = 4
FIRST_PAGES = 5


def step_kernel(
    n,
    counts,
    fill,
    order,
    routes,
    queries,
    new_kv,
    kv_pool,
    hidden,
    weight,
    sectioned,
    gathered,
    arrival,
    sect_v,
    outgoing,
    q_raw,
    q_rows,
    new_raw,
    new_rows,
    kv_v,
    hidden_v,
    weight_v,
    attn_rows,
    attn_v,
    terms,
    landed,
    load_sems,
    kv_sems,
    weight_sems,
    own_sems,
    page_send,
    page_recv,
    term_send,
    term_recv,
    block_send,
    block_recv,
):
    me = lax.axis_index("heads")
    slots, pool_pages, page_size, width = kv_v.shape
    head_dim = width // 2
    requests = q_raw.shape[0]
    group = q_rows.shape[2]
    pages = sect_v.shape[0] - 1
    cap = outgoing.shape[2]
    block = terms.shape[2]
    chunk_total, _, chunk = weight_v.shape
    chunks = block // chunk

    bits = [1 << s for s in range(n.bit_length() - 1)]

    def partner(mask):
        place = me
        for bit in bits:
            if mask & bit:
                place = place + bit * (1 - 2 * lax.rem(me // bit, 2))
        return place

    def lowest(mask):
        return mask & -mask if mask else n

    masks = sorted(range(n), key=lambda mask: (lowest(mask), -mask))
    far = [mask for mask in range(n - 1, 0, -1) if mask & (n // 2)]
    near = [mask for mask in range(n - 1, 0, -1) if not mask & (n // 2)]

    loads = [
        pltpu.make_async_copy(src, dst, load_sems.at[i])
        for i, (src, dst) in enumerate(
            (
                (sectioned.at[0, 0], sect_v.at[pl.ds(0, pages)]),
                (queries, q_raw),
                (new_kv, new_raw),
                (hidden, hidden_v),
            )
        )
    ]
    for load in loads[:3]:
        load.start()
    kv_loads = [
        pltpu.make_async_copy(kv_pool.at[l], kv_v.at[l], kv_sems.at[l]) for l in range(slots)
    ]
    for load in kv_loads:
        load.start()

    def weight_load(i):
        column = partner(masks[i // chunks]) * block + (i % chunks) * chunk
        return pltpu.make_async_copy(
            weight.at[:, pl.ds(pl.multiple_of(column, chunk), chunk)],
            weight_v.at[i],
            weight_sems.at[i],
        )

    for load in loads[3:]:
        load.start()
    for i in range(chunk_total):
        weight_load(i).start()

    barrier = pltpu.get_barrier_semaphore()
    for mask in range(1, n):
        pl.semaphore_signal(
            barrier, inc=1, device_id={"heads": partner(mask)}, device_id_type=MESH
        )

    sect_v[pages] = jnp.zeros(sect_v.shape[1:], sect_v.dtype)
    loads[0].wait()
    page_heads = [routes[0, j] for j in range(pages)]

    def fill_outgoing(mask, l):
        head = (partner(mask) * slots + l) * KV_HEADS // (n * slots)
        found = jnp.int32(0)
        picks = [jnp.int32(pages)] * cap
        for j in range(pages):
            hit = page_heads[j] == head
            for k in range(cap):
                picks[k] = jnp.where(hit & (found == k), j, picks[k])
            found = found + jnp.where(hit, 1, 0)
        for k in range(cap):
            outgoing[mask, l, k] = sect_v[picks[k]]

    def page_copy(mask, l, k, place):
        return pltpu.make_async_remote_copy(
            src_ref=outgoing.at[mask, l, k],
            dst_ref=arrival.at[l, 0, place, k],
            send_sem=page_send.at[mask, l, k],
            recv_sem=page_recv.at[mask, l, k],
            device_id={"heads": partner(mask)},
            device_id_type=MESH,
        )

    far_pages = [(mask, l, k) for l in range(slots) for mask in far for k in range(cap)]
    first_count = len(far_pages) * FIRST_PAGES // 8
    waiting = far_pages[first_count:]

    def send_waiting(count):
        for spot in waiting[:count]:
            page_copy(*spot, me).start()
        del waiting[:count]

    filled = set()
    for spot in far_pages[:first_count]:
        if spot[:2] not in filled:
            filled.add(spot[:2])
            fill_outgoing(*spot[:2])
        if len(filled) == 1 and spot == far_pages[0]:
            pl.semaphore_wait(barrier, n - 1)
        page_copy(*spot, me).start()
    for mask in near:
        for l in range(slots):
            fill_outgoing(mask, l)
            for k in range(cap):
                page_copy(mask, l, k, me).start()
    for mask in [*far, 0]:
        for l in range(slots):
            if (mask, l) not in filled:
                fill_outgoing(mask, l)
    own_copies = [
        pltpu.make_async_copy(outgoing.at[0, l], arrival.at[l, 0, me], own_sems.at[l])
        for l in range(slots)
    ]
    for copy in own_copies:
        copy.start()

    loads[1].wait()
    loads[2].wait()
    new_rows[...] = new_raw[...].astype(jnp.float32)
    for l in range(slots):
        for g in range(group):
            first = (l * group + g) * head_dim
            q_rows[l, :, g, :] = q_raw[:, first : first + head_dim].astype(jnp.float32)
    for load in kv_loads:
        load.wait()

    score_scale = 1.0 / head_dim**0.5

    def attend(i, start):
        chains = []
        for sub in range(UNROLL):
            r = i * UNROLL + sub
            count = counts[0, r]
            context = (count - 1) * page_size + fill[0, r]
            picked = [
                order[0, jnp.minimum(start + j, pool_pages - 1)] for j in range(MAX_PAGES)
            ]
            start = start + count
            chains += [(l, r, context, picked) for l in range(slots)]
        shape = (group, MAX_PAGES * page_size)
        token = lax.broadcasted_iota(jnp.int32, shape, 1)
        raw = []
        for l, r, context, picked in chains:
            keys = jnp.concatenate([kv_v[l, p, :, :head_dim] for p in picked], axis=0)
            raw.append(
                lax.dot_general(
                    q_rows[l, r].astype(jnp.bfloat16),
                    keys,
                    (((1,), (1,)), ((), ())),
                    preferred_element_type=jnp.float32,
                )
            )
        fresh_scores = [
            jnp.sum(q_rows[l, r] * new_rows[l, pl.ds(r, 1), :][:, :head_dim], axis=1, keepdims=True)
            * score_scale
            for l, r, context, picked in chains
        ]
        scores = [
            jnp.where(token < chain[2], value * score_scale, -1e30)
            for chain, value in zip(chains, raw)
        ]
        tops = [
            jnp.maximum(jnp.max(value, axis=1, keepdims=True), fresh)
            for value, fresh in zip(scores, fresh_scores)
        ]
        ws = [
            jnp.where(token < chain[2], jnp.exp(value - top), 0.0)
            for chain, value, top in zip(chains, scores, tops)
        ]
        fresh_ws = [jnp.exp(fresh - top) for fresh, top in zip(fresh_scores, tops)]
        nums = []
        for (l, r, context, picked), w in zip(chains, ws):
            values = jnp.concatenate([kv_v[l, p, :, head_dim:] for p in picked], axis=0)
            nums.append(
                jnp.dot(w.astype(jnp.bfloat16), values, preferred_element_type=jnp.float32)
            )
        dens = [
            jnp.sum(w, axis=1, keepdims=True) + fresh for w, fresh in zip(ws, fresh_ws)
        ]
        for (l, r, context, picked), num, den, fresh in zip(chains, nums, dens, fresh_ws):
            rounded = fresh.astype(jnp.bfloat16).astype(jnp.float32)
            num = num + rounded * new_rows[l, pl.ds(r, 1), :][:, head_dim:]
            attn_rows[l, r] = num / den
        return start

    lax.fori_loop(0, requests // UNROLL, attend, jnp.int32(0))
    for l in range(slots):
        for g in range(group):
            first = (l * group + g) * head_dim
            attn_v[:, first : first + head_dim] = attn_rows[l, :, g, :].astype(jnp.bfloat16)

    def term_copy(mask):
        return pltpu.make_async_remote_copy(
            src_ref=terms.at[mask],
            dst_ref=landed.at[mask],
            send_sem=term_send.at[mask],
            recv_sem=term_recv.at[mask],
            device_id={"heads": partner(lowest(mask))},
            device_id_type=MESH,
        )

    def block_copy(mask, place):
        return pltpu.make_async_remote_copy(
            src_ref=gathered.at[place],
            dst_ref=gathered.at[place],
            send_sem=block_send.at[mask],
            recv_sem=block_recv.at[mask],
            device_id={"heads": partner(lowest(mask))},
            device_id_type=MESH,
        )

    quarter = -(-len(waiting) // 3)
    for i, mask in enumerate(masks):
        parts = []
        for part in range(chunks):
            weight_load(i * chunks + part).wait()
            parts.append(
                jnp.dot(
                    attn_v[...], weight_v[i * chunks + part], preferred_element_type=jnp.float32
                )
            )
        total = parts[0] if chunks == 1 else jnp.concatenate(parts, axis=1)
        if mask == 0:
            loads[3].wait()
            column = pl.multiple_of(me * block, block)
            total = total + hidden_v[:, pl.ds(column, block)].astype(jnp.float32)
        for bit in bits:
            if bit < lowest(mask):
                term_copy(mask + bit).wait_recv()
                total = total + landed[mask + bit].astype(jnp.float32)
        if mask:
            terms[mask] = total.astype(jnp.bfloat16)
            term_copy(mask).start()
            if i == n - 2:
                send_waiting(quarter)
        else:
            gathered[me] = total.astype(jnp.bfloat16)

    for bit in reversed(bits):
        block_copy(bit, me).start()
        if bit == bits[-1]:
            send_waiting(quarter)
    for bit in reversed(bits):
        for mask in range(1, n):
            if lowest(mask) == bit:
                block_copy(mask, partner(mask)).wait_recv()
                for lower in bits:
                    if lower < bit:
                        block_copy(mask + lower, partner(mask)).start()
        if bit == bits[-1]:
            send_waiting(len(waiting))

    for mask in range(1, n):
        term_copy(mask).wait_send()
        block_copy(mask, me).wait_send()
        for l in range(slots):
            for k in range(cap):
                page_copy(mask, l, k, me).wait_send()
                page_copy(mask, l, k, partner(mask)).wait_recv()
    for copy in own_copies:
        copy.wait()


def finish_kernel(gathered, gain, landed, residual_out, normed_out, arrival, held, sems):
    n, requests, block = gathered.shape
    slots = held.shape[0]
    into = [pltpu.make_async_copy(landed.at[l], held.at[l], sems.at[0, l]) for l in range(slots)]
    out = [pltpu.make_async_copy(held.at[l], arrival.at[l], sems.at[1, l]) for l in range(slots)]
    for copy in into:
        copy.start()
    square = jnp.zeros((requests, 1), jnp.float32)
    for c in range(n):
        mixed = gathered[c].astype(jnp.float32)
        square = square + jnp.sum(mixed * mixed, axis=1, keepdims=True)
    factor = lax.rsqrt(square / (n * block) + norm_epsilon)
    for l in range(slots):
        into[l].wait()
        out[l].start()
    for c in range(n):
        piece = gathered[c]
        here = slice(c * block, (c + 1) * block)
        residual_out[:, here] = piece
        scale = gain[here].astype(jnp.float32).reshape(1, block)
        normed_out[:, here] = (piece.astype(jnp.float32) * factor * scale).astype(jnp.bfloat16)
    for copy in out:
        copy.wait()


def per_device(
    queries,
    new_kv,
    kv_pool,
    page_counts,
    last_fill,
    page_order,
    hidden,
    out_weight,
    norm_gain,
    sectioned,
    routes,
    *,
    cap,
):
    n = lax.axis_size("heads")
    slots, pool_pages, page_size, width = kv_pool.shape
    head_dim = width // 2
    requests, model = hidden.shape
    rows = out_weight.shape[0]
    group = rows // (slots * head_dim)
    pages = sectioned.shape[2]
    block = model // n
    chunk = min(CHUNK, block)
    bf16, f32 = jnp.bfloat16, jnp.float32
    dma = pltpu.SemaphoreType.DMA
    smem = pl.BlockSpec(memory_space=pltpu.SMEM)
    hbm = pl.BlockSpec(memory_space=pl.ANY)
    vmem = pl.BlockSpec(memory_space=pltpu.VMEM)
    landing = jax.ShapeDtypeStruct((slots, 1, n, cap, page_size, width), bf16)
    gathered, landed = pl.pallas_call(
        functools.partial(step_kernel, n),
        out_shape=(jax.ShapeDtypeStruct((n, requests, block), bf16), landing),
        in_specs=[smem] * 4 + [hbm] * 6,
        out_specs=(vmem, hbm),
        scratch_shapes=[
            pltpu.VMEM((pages + 1, page_size, width), bf16),
            pltpu.VMEM((n, slots, cap, page_size, width), bf16),
            pltpu.VMEM((requests, rows), bf16),
            pltpu.VMEM((slots, requests, group, head_dim), f32),
            pltpu.VMEM((slots, requests, width), bf16),
            pltpu.VMEM((slots, requests, width), f32),
            pltpu.VMEM((slots, pool_pages, page_size, width), bf16),
            pltpu.VMEM((requests, model), bf16),
            pltpu.VMEM((model // chunk, rows, chunk), bf16),
            pltpu.VMEM((slots, requests, group, head_dim), f32),
            pltpu.VMEM((requests, rows), bf16),
            pltpu.VMEM((n, requests, block), bf16),
            pltpu.VMEM((n, requests, block), bf16),
            dma((4,)),
            dma((slots,)),
            dma((model // chunk,)),
            dma((slots,)),
            dma((n, slots, cap)),
            dma((n, slots, cap)),
            dma((n,)),
            dma((n,)),
            dma((n,)),
            dma((n,)),
        ],
        compiler_params=pltpu.CompilerParams(
            collective_id=0, has_side_effects=True, vmem_limit_bytes=60 * 1024 * 1024
        ),
        name="decode_step",
    )(
        page_counts,
        last_fill,
        page_order,
        routes.reshape(1, pages),
        queries,
        new_kv,
        kv_pool,
        hidden,
        out_weight,
        sectioned,
    )
    return pl.pallas_call(
        finish_kernel,
        out_shape=(
            jax.ShapeDtypeStruct((requests, model), bf16),
            jax.ShapeDtypeStruct((requests, model), bf16),
            landing,
        ),
        in_specs=[vmem, vmem, hbm],
        out_specs=(vmem, vmem, hbm),
        scratch_shapes=[pltpu.VMEM(landing.shape, bf16), dma((2, slots))],
        name="finish",
    )(gathered, norm_gain, landed)


PER_HEAD_CAP = 2


def solution(mesh):
    return jax.shard_map(
        functools.partial(per_device, cap=PER_HEAD_CAP),
        mesh=mesh,
        in_specs=(
            P(("groups", "batch"), "heads"),
            P(("groups", "heads"), "batch", None),
            P(("groups", "heads"), "batch", None, None),
            P(("groups", "batch"), None),
            P(("groups", "batch"), None),
            P(("groups", "batch"), None),
            P(("groups", "batch"), None),
            P("heads", None),
            P(),
            P(("groups", "heads"), "batch", None, None, None),
            P(("groups", "heads"), "batch", None, None),
        ),
        out_specs=(
            P(("groups", "batch"), None),
            P(("groups", "batch"), None),
            P(("groups", "heads"), "batch", None, None, None, None),
        ),
        check_vma=False,
    )
```

time: 52.6 us -> 47.3 us (0.90)
  local copies, waits for them, and re-layouts: 6.98 us -> 0 us
  Pallas kernels: 44.7 us -> 46.5 us
    unnamed x3 -> x0, local copies, waits for them, and re-layouts: 5.62 us -> none
    pallas_call x0 -> x1, Pallas kernels: none -> 3.78 us  [per_device(): pl.pallas_call(finish_kernel, out_shape=(jax.ShapeDtypeStruct((requests,...]
    pallas_call x1, Pallas kernels: 44.7 us -> 42.7 us  [per_device(): pl.pallas_call(functools.partial(step_kernel, n), out_shape=(jax.ShapeDty...]
    reshape x1 -> x0, local copies, waits for them, and re-layouts: 1.35 us -> none  [per_device(): norm_gain.reshape(1, model)]
where the time goes in v2:
time: 47.3 us; the launch traced here: 47.1 us
  Pallas kernels  46.5 us (98%)
  between operations  0.64 us (1%)
    pallas_call x1, Pallas kernels, per_device(): pl.pallas_call(functools.partial(step_kernel, n), out_shape=(jax.ShapeDty...  42.7 us
    pallas_call x1, Pallas kernels, per_device(): pl.pallas_call(finish_kernel, out_shape=(jax.ShapeDtypeStruct((requests,...  3.78 us

profile of v2, /device:TPU:0, one launch (start us, length us, event | category | flops | bytes accessed | tf_op | source)
XLA Modules:
  0.0 47.1 jit_solution(3495905263493095606)
XLA Ops:
  0.6 42.7 %decode_step.1 = (bf16[4,16,2048]{2,1,0:T(8,128)(2,1)}, bf16[2,1,4,2,128,256]{5,4,3,2,1,0:T(8,128)(2,1)}) custom-call(s32[1,16]{1,0:T(1,128)} %counts.1, s32[1,16]{1,0:T(1,128)} %fill.1, s32[1,48]{1,0:T(1,128)} %order.1, s32[1,8]{1,0:T(1,128)} %bitcast.1, bf16[16,2048]{1,0:T(8,128)(2,1)} %queries.1, bf16[2,16,256]{2,1,0:T(8,128)(2,1)} %new_kv.1, ...), custom_call_target="tpu_custom_call" | custom-call | tf_op jit(solution)/shard_map/decode_step/pallas_call | solution.py:384
  43.3 3.8 %finish.1 = (bf16[16,8192]{1,0:T(8,128)(2,1)}, bf16[16,8192]{1,0:T(8,128)(2,1)}, bf16[2,1,4,2,128,256]{5,4,3,2,1,0:T(8,128)(2,1)}) custom-call(bf16[4,16,2048]{2,1,0:T(8,128)(2,1)} %get-tuple-element.5.gathered, bf16[8192]{0:T(1024)(128)(2,1)} %gain.1, bf16[2,1,4,2,128,256]{5,4,3,2,1,0:T(8,128)(2,1)} %get-tuple-element.6.landed), custom_call_target="tpu_custom_call" | custom-call | tf_op jit(solution)/shard_map/finish/pallas_call | solution.py:430

commit v3 on v2

--- a/solution.py
+++ b/solution.py
@@ -155,19 +155,19 @@
             page_copy(*spot, me).start()
         del waiting[:count]
 
+    for i, mask in enumerate(near):
+        for l in range(slots):
+            fill_outgoing(mask, l)
+            if i == 0 and l == 0:
+                pl.semaphore_wait(barrier, n - 1)
+            for k in range(cap):
+                page_copy(mask, l, k, me).start()
     filled = set()
     for spot in far_pages[:first_count]:
         if spot[:2] not in filled:
             filled.add(spot[:2])
             fill_outgoing(*spot[:2])
-        if len(filled) == 1 and spot == far_pages[0]:
-            pl.semaphore_wait(barrier, n - 1)
         page_copy(*spot, me).start()
-    for mask in near:
-        for l in range(slots):
-            fill_outgoing(mask, l)
-            for k in range(cap):
-                page_copy(mask, l, k, me).start()
     for mask in [*far, 0]:
         for l in range(slots):
             if (mask, l) not in filled:
@@ -326,13 +326,23 @@
         copy.wait()
 
 
-def finish_kernel(gathered, gain, landed, residual_out, normed_out, arrival, held, sems):
+def finish_kernel(
+    gathered_in, gain_in, landed, residual_out, normed_out, arrival, held, gathered, gain, sems, in_sems
+):
     n, requests, block = gathered.shape
+    loads = [
+        pltpu.make_async_copy(gathered_in, gathered, in_sems.at[0]),
+        pltpu.make_async_copy(gain_in, gain, in_sems.at[1]),
+    ]
+    for load in loads:
+        load.start()
     slots = held.shape[0]
     into = [pltpu.make_async_copy(landed.at[l], held.at[l], sems.at[0, l]) for l in range(slots)]
     out = [pltpu.make_async_copy(held.at[l], arrival.at[l], sems.at[1, l]) for l in range(slots)]
     for copy in into:
         copy.start()
+    for load in loads:
+        load.wait()
     square = jnp.zeros((requests, 1), jnp.float32)
     for c in range(n):
         mixed = gathered[c].astype(jnp.float32)
@@ -434,9 +444,15 @@
             jax.ShapeDtypeStruct((requests, model), bf16),
             landing,
         ),
-        in_specs=[vmem, vmem, hbm],
+        in_specs=[hbm, hbm, hbm],
         out_specs=(vmem, vmem, hbm),
-        scratch_shapes=[pltpu.VMEM(landing.shape, bf16), dma((2, slots))],
+        scratch_shapes=[
+            pltpu.VMEM(landing.shape, bf16),
+            pltpu.VMEM((n, requests, block), bf16),
+            pltpu.VMEM((model,), bf16),
+            dma((2, slots)),
+            dma((2,)),
+        ],
         name="finish",
     )(gathered, norm_gain, landed)
 

time: 47.3 us -> 46.4 us (0.981)
  Pallas kernels: 46.5 us -> 45.6 us
    pallas_call x1, Pallas kernels: 3.78 us -> 2.93 us  [per_device(): pl.pallas_call(finish_kernel, out_shape=(jax.ShapeDtypeStruct((requests,...]
where the time goes in v3:
time: 46.4 us; the launch traced here: 46.2 us
  Pallas kernels  45.6 us (98%)
  between operations  0.64 us (1%)
    pallas_call x1, Pallas kernels, per_device(): pl.pallas_call(functools.partial(step_kernel, n), out_shape=(jax.ShapeDty...  42.6 us
    pallas_call x1, Pallas kernels, per_device(): pl.pallas_call(finish_kernel, out_shape=(jax.ShapeDtypeStruct((requests,...  2.93 us

profile of v3, /device:TPU:0, one launch (start us, length us, event | category | flops | bytes accessed | tf_op | source)
XLA Modules:
  0.0 46.2 jit_solution(7121847085907726386)
XLA Ops:
  0.6 42.6 %decode_step.1 = (bf16[4,16,2048]{2,1,0:T(8,128)(2,1)}, bf16[2,1,4,2,128,256]{5,4,3,2,1,0:T(8,128)(2,1)}) custom-call(s32[1,16]{1,0:T(1,128)} %counts.1, s32[1,16]{1,0:T(1,128)} %fill.1, s32[1,48]{1,0:T(1,128)} %order.1, s32[1,8]{1,0:T(1,128)} %bitcast.1, bf16[16,2048]{1,0:T(8,128)(2,1)} %queries.1, bf16[2,16,256]{2,1,0:T(8,128)(2,1)} %new_kv.1, ...), custom_call_target="tpu_custom_call" | custom-call | tf_op jit(solution)/shard_map/decode_step/pallas_call | solution.py:394
  43.3 2.9 %finish.1 = (bf16[16,8192]{1,0:T(8,128)(2,1)}, bf16[16,8192]{1,0:T(8,128)(2,1)}, bf16[2,1,4,2,128,256]{5,4,3,2,1,0:T(8,128)(2,1)}) custom-call(bf16[4,16,2048]{2,1,0:T(8,128)(2,1)} %get-tuple-element.5.gathered_in, bf16[8192]{0:T(1024)(128)(2,1)} %gain_in.1, bf16[2,1,4,2,128,256]{5,4,3,2,1,0:T(8,128)(2,1)} %get-tuple-element.6.landed), custom_call_target="tpu_custom_call" | custom-call | tf_op jit(solution)/shard_map/finish/pallas_call | solution.py:440
